TPU v7x, 32 devices: a whole 2x2x4 slice. The times are simulated.
32 devices in a mesh: row: 8 (over z, y), col: 4 (over x, core).
Axes of the slice: x: 2, y: 2, z: 4, core: 2. Of those that a mesh axis runs over, the one named last changes fastest.
Arguments:
- new_dosage: float32 [4096, 1024], P(('col', 'row')), may hold values from 0 to 2
- old_dosage: float32 [16384, 1024], P(('row', 'col')), may hold values from 0 to 2
- grm: bfloat16 [16384, 4096], P('row', 'col'), may hold values from -1.5 to 1.5
- counts: int32 [8], P('col'), may hold values from 256 to 512
- affected: int32 [32, 8], P('row', 'col'), may hold values from 0 to 1, as said below
Outputs:
- updated: bfloat16 [16384, 4096], P('row', 'col')
Inputs may be any that keep to these rules, and one draw needn't show every extreme that they name: `affected`: the density of marked tile pairs differs from one tile of new samples to the next.
All inputs are finite; a program needn't handle non-finite values.
Results may differ from a plain program's by a relative error of at most 0.00115.
Values may be sent and summed in bfloat16 or wider, within the bound.
A program may use at most 128 MiB of HBM per device.

v0:
```python
import jax
import jax.numpy as jnp
from jax import lax
from jax.sharding import PartitionSpec as P

TILE = 512


def on_device(new_dosage, old_dosage, grm, counts, affected):
    devices = lax.axis_size("row") * lax.axis_size("col")
    totals = lax.psum(jnp.sum(old_dosage, axis=0), ("row", "col"))
    doubled = totals / (old_dosage.shape[0] * devices)
    spread = jnp.sqrt(doubled * (1.0 - 0.5 * doubled) + 0.1)
    usable = (jnp.arange(TILE)[None, :] < counts[:, None]).reshape(-1).astype(jnp.float32)
    snp_count = new_dosage.shape[1]
    contract = (((1,), (1,)), ((), ()))
    local_rows = new_dosage.shape[0]
    usable_mine = lax.dynamic_slice_in_dim(usable, lax.axis_index("row") * local_rows, local_rows)
    scores_mine = ((new_dosage - doubled) / spread * usable_mine[:, None]).astype(jnp.bfloat16)
    new_scores = lax.all_gather(scores_mine, "row", axis=0, tiled=True)
    old_mine = ((old_dosage - doubled) / spread).astype(jnp.bfloat16)
    product = lax.dot_general(
        lax.all_gather(old_mine, "col", axis=0, tiled=True),
        new_scores,
        contract,
        preferred_element_type=jnp.float32,
    )
    row_count, col_count = product.shape
    scaled = (product / snp_count).reshape(row_count // TILE, TILE, col_count // TILE, TILE)
    masked_update = scaled * affected.astype(jnp.float32)[:, None, :, None]
    return (grm.astype(jnp.float32) + masked_update.reshape(row_count, col_count)).astype(
        jnp.bfloat16
    )


def solution(mesh):
    in_specs = (
        P(("col", "row"), None),
        P(("row", "col"), None),
        P("row", "col"),
        P("col"),
        P("row", "col"),
    )
    out_specs = P("row", "col")
    return jax.shard_map(
        on_device, mesh=mesh, in_specs=in_specs, out_specs=out_specs, check_vma=False
    )
```

profile of v0, /device:TPU:0, one launch (start us, length us, event | category | flops | bytes accessed | tf_op | source)
XLA Modules:
  0.0 157.1 jit_solution(6402705490686522627)
XLA Ops:
  6.5 0.0 copy-start
  6.5 0.0 copy-start.1
  6.5 0.0 all-gather.5.cloned.1.call-start
  6.5 1.9 %reduce_sum.9 = f32[1024]{0:T(1024)S(1)} reduce(f32[512,1024]{1,0:T(8,128)} %param.6, f32[]{:T(128)} %constant.5.clone.1), dimensions={0}, to_apply=%region_0.0 | reduce | flops 523264 | bytes 2101252 | tf_op jit(solution)/shard_map/reduce_sum | solution.py:11
  8.4 42.0 %psum.7 = f32[1024]{0:T(1024)S(1)} all-reduce(f32[1024]{0:T(1024)S(1)} %reduce_sum.9), channel_id=1, replica_groups=mesh['row'=8,'col'=4] {'row','col'}, use_global_device_ids=true, to_apply=%region_1.0 | all-reduce | flops 1024 | bytes 8192 | tf_op jit(solution)/shard_map/psum | solution.py:11
  50.5 0.7 fusion
  51.2 0.1 dynamic_slice.3
  51.3 1.8 %multiply_convert_fusion = bf16[128,1024]{1,0:T(8,128)(2,1)} fusion(f32[128,1024]{1,0:T(8,128)} %param.5, f32[128]{0:T(128)S(1)} %dynamic_slice.3, f32[1024]{0:T(1024)S(1)} %get-tuple-element.6, f32[1024]{0:T(1024)S(1)} %get-tuple-element.5), kind=kLoop, calls=%fused_computation.2 | loop fusion | flops 524288 | bytes 795136 | tf_op jit(solution)/shard_map/convert_element_type | solution.py:19
  53.1 0.0 all-gather.5.cloned.1.call-update
  53.1 0.0 all-gather.3.cloned.1.call-start
  53.2 0.0 copy-done
  53.2 1.3 divide_convert_fusion
  54.5 0.0 all-gather.3.cloned.1.call-update
  54.5 0.0 copy-done.1
  54.5 0.1 copy.6
  54.6 5.5 %mul.37 = f32[4,512,2,512]{3,2,1,0:T(2,128)} broadcast(f32[4,2]{1,0:T(4,128)S(1)} %copy.6), dimensions={0,2} | broadcast | bytes 8388640 | tf_op jit(solution)/shard_map/mul | solution.py:30
  60.1 8.9 %copy.8 = f32[256,8,2,512]{3,1,2,0:T(8,128)} copy(f32[256,8,2,512]{3,2,1,0:T(2,128)} %bitcast.8) | data formatting | bytes 16777216
  68.9 33.3 %all-gather.5.cloned.1.call-done = bf16[1024,1024]{1,0:T(8,128)(2,1)} async-done(((bf16[128,1024]{1,0:T(8,128)(2,1)}), bf16[1024,1024]{1,0:T(8,128)(2,1)}) %all-gather.5.cloned.1.call-update) | async-done | bytes 2097168 | tf_op jit(solution)/shard_map/all_gather | solution.py:20
  102.2 34.6 %all-gather.3.cloned.1.call-done = bf16[2048,1024]{1,0:T(8,128)(2,1)} async-done(((bf16[512,1024]{1,0:T(8,128)(2,1)}), bf16[2048,1024]{1,0:T(8,128)(2,1)}) %all-gather.3.cloned.1.call-update) | async-done | bytes 4194320 | tf_op jit(solution)/shard_map/all_gather | solution.py:23
  136.8 13.5 %add_convert_fusion = bf16[2048,1024]{1,0:T(8,128)(2,1)} fusion(f32[2048,1024]{1,0:T(8,128)} %bitcast.9, bf16[2048,1024]{1,0:T(8,128)(2,1)} %param.7, bf16[2048,1024]{1,0:T(8,128)(2,1)} %all-gather.3.cloned.1.call-done, bf16[1024,1024]{1,0:T(8,128)(2,1)} %all-gather.5.cloned.1.call-done), kind=kOutput, calls=%fused_computation | convolution fusion | flops 4305453056 | bytes 23068672 | tf_op jit(solution)/shard_map/dot_general | solution.py:22
  (3 shorter events, 0.0 us)
Async XLA Ops:
  6.5 46.7 %copy-start = (f32[512,1024]{1,0:T(8,128)S(1)}, f32[512,1024]{1,0:T(8,128)}, u32[]{:S(2)}) copy-start(f32[512,1024]{1,0:T(8,128)} %param.6) | copy-start | bytes 6291460
  6.5 48.0 %copy-start.1 = (s32[4,2]{0,1:T(2,128)S(1)}, s32[4,2]{0,1:T(2,128)}, u32[]{:S(2)}) copy-start(s32[4,2]{0,1:T(2,128)} %param.9) | copy-start | bytes 100
  6.5 95.6 %all-gather.5.cloned.1.call-start = ((), (), s32[]{:S(2)}) async-start(), calls=%async_computation.1 | async-start | bytes 2359296 | tf_op jit(solution)/shard_map/all_gather | solution.py:20
  53.1 83.6 %all-gather.3.cloned.1.call-start = ((), (), s32[]{:S(2)}) async-start(), calls=%async_computation | async-start | bytes 5242880 | tf_op jit(solution)/shard_map/all_gather | solution.py:23
Sparse Core Ops, SparseCore 0:
  53.3 48.8 all-gather.4
  103.7 32.9 all-gather.2
where the time goes:
time: 157 us
  waiting for transfers between devices  67.9 us (43%)
  blocking collectives  42 us (27%)
  local copies, waits for them, and re-layouts  14.5 us (9%)
  matrix products  13.5 us (9%)
  between operations  13.4 us (9%)
  other arithmetic  5.75 us (4%)
    psum x1, blocking collectives, on_device(): totals = lax.psum(jnp.sum(old_dosage, axis=0), ('row', 'col'))  42 us
    all_gather x1, waiting for transfers between devices, on_device(): lax.all_gather(old_mine, 'col', axis=0, tiled=True)  34.6 us
    all_gather x1, waiting for transfers between devices, on_device(): new_scores = lax.all_gather(scores_mine, 'row', axis=0, tiled=True)  33.3 us
    dot_general x1, matrix products, on_device(): lax.dot_general(lax.all_gather(old_mine, 'col', axis=0, tiled=True), new_...  13.5 us
    unnamed x6, local copies, waits for them, and re-layouts  8.87 us
    mul x1, local copies, waits for them, and re-layouts, on_device(): masked_update = scaled * affected.astype(jnp.float32)[:, None, :, None]  5.45 us
  transfers between devices with their start and end apart: 2, of which 2 were waited for; matrix products, arithmetic and copies ran while one was open for 10% of the time, Pallas kernels for 0%

commit v1 on v0

--- a/solution.py
+++ b/solution.py
@@ -8,7 +8,7 @@
 
 def on_device(new_dosage, old_dosage, grm, counts, affected):
     devices = lax.axis_size("row") * lax.axis_size("col")
-    totals = lax.psum(jnp.sum(old_dosage, axis=0), ("row", "col"))
+    totals = jnp.sum(lax.all_gather(jnp.sum(old_dosage, axis=0), ("row", "col")), axis=0)
     doubled = totals / (old_dosage.shape[0] * devices)
     spread = jnp.sqrt(doubled * (1.0 - 0.5 * doubled) + 0.1)
     usable = (jnp.arange(TILE)[None, :] < counts[:, None]).reshape(-1).astype(jnp.float32)

time: 157 us -> 155 us (0.987)
  waiting for transfers between devices: 67.9 us -> 64.3 us
  blocking collectives: 42 us -> 43.6 us
    all_gather x0 -> x1, blocking collectives: none -> 43.6 us  [on_device(): lax.all_gather(jnp.sum(old_dosage, axis=0), ('row', 'col'))]
    psum x1 -> x0, blocking collectives: 42 us -> none  [on_device(): totals = lax.psum(jnp.sum(old_dosage, axis=0), ('row', 'col'))]
    all_gather x1, waiting for transfers between devices: 33.3 us -> 29.7 us  [on_device(): new_scores = lax.all_gather(scores_mine, 'row', axis=0, tiled=True)]
where the time goes in v1:
time: 155 us
  waiting for transfers between devices  64.3 us (41%)
  blocking collectives  43.6 us (28%)
  local copies, waits for them, and re-layouts  14.4 us (9%)
  matrix products  13.5 us (9%)
  between operations  13.4 us (9%)
  other arithmetic  5.77 us (4%)
    all_gather x1, blocking collectives, on_device(): lax.all_gather(jnp.sum(old_dosage, axis=0), ('row', 'col'))  43.6 us
    all_gather x1, waiting for transfers between devices, on_device(): lax.all_gather(old_mine, 'col', axis=0, tiled=True)  34.6 us
    all_gather x1, waiting for transfers between devices, on_device(): new_scores = lax.all_gather(scores_mine, 'row', axis=0, tiled=True)  29.7 us
    dot_general x1, matrix products, on_device(): lax.dot_general(lax.all_gather(old_mine, 'col', axis=0, tiled=True), new_...  13.5 us
    unnamed x6, local copies, waits for them, and re-layouts  8.71 us
    mul x1, local copies, waits for them, and re-layouts, on_device(): masked_update = scaled * affected.astype(jnp.float32)[:, None, :, None]  5.45 us
  transfers between devices with their start and end apart: 2, of which 2 were waited for; matrix products, arithmetic and copies ran while one was open for 10% of the time, Pallas kernels for 0%

profile of v1, /device:TPU:0, one launch (start us, length us, event | category | flops | bytes accessed | tf_op | source)
XLA Modules:
  0.0 155.0 jit_solution(9454500989902597892)
XLA Ops:
  6.5 0.0 copy-start
  6.5 0.0 copy-start.1
  6.5 0.0 all-gather.6.cloned.1.call-start
  6.5 1.9 %reduce_sum.18 = f32[1024]{0:T(1024)S(1)} reduce(f32[512,1024]{1,0:T(8,128)} %param.6, f32[]{:T(128)} %constant.5.clone.1), dimensions={0}, to_apply=%region_0.0 | reduce | flops 523264 | bytes 2101252 | tf_op jit(solution)/shard_map/reduce_sum | solution.py:11
  8.4 43.6 %all-gather = f32[32768]{0:T(1024)S(1)} all-gather(f32[1024]{0:T(1024)S(1)} %reduce_sum.18), channel_id=2, replica_groups=mesh['row'=8,'col'=4] {'row','col'}, dimensions={0}, use_global_device_ids=true | all-gather | bytes 135168 | tf_op jit(solution)/shard_map/all_gather | solution.py:11
  52.1 0.7 fusion
  52.8 0.1 dynamic_slice.3
  52.9 1.8 %multiply_convert_fusion = bf16[128,1024]{1,0:T(8,128)(2,1)} fusion(f32[128,1024]{1,0:T(8,128)} %param.5, f32[128]{0:T(128)S(1)} %dynamic_slice.3, f32[1024]{0:T(1024)S(1)} %get-tuple-element.6, f32[1024]{0:T(1024)S(1)} %get-tuple-element.5), kind=kLoop, calls=%fused_computation.2 | loop fusion | flops 524288 | bytes 795136 | tf_op jit(solution)/shard_map/convert_element_type | solution.py:19
  54.8 0.0 all-gather.6.cloned.1.call-update
  54.8 0.0 all-gather.4.cloned.1.call-start
  54.8 0.0 copy-done
  54.8 1.3 divide_convert_fusion
  56.1 0.0 all-gather.4.cloned.1.call-update
  56.1 0.0 copy-done.1
  56.2 0.1 copy.8
  56.3 5.5 %mul.45 = f32[4,512,2,512]{3,2,1,0:T(2,128)} broadcast(f32[4,2]{1,0:T(4,128)S(1)} %copy.8), dimensions={0,2} | broadcast | bytes 8388640 | tf_op jit(solution)/shard_map/mul | solution.py:30
  61.7 8.7 %copy.10 = f32[256,8,2,512]{3,1,2,0:T(8,128)} copy(f32[256,8,2,512]{3,2,1,0:T(2,128)} %bitcast.8) | data formatting | bytes 16777216
  70.4 29.7 %all-gather.6.cloned.1.call-done = bf16[1024,1024]{1,0:T(8,128)(2,1)} async-done(((bf16[128,1024]{1,0:T(8,128)(2,1)}), bf16[1024,1024]{1,0:T(8,128)(2,1)}) %all-gather.6.cloned.1.call-update) | async-done | bytes 2097168 | tf_op jit(solution)/shard_map/all_gather | solution.py:20
  100.1 34.6 %all-gather.4.cloned.1.call-done = bf16[2048,1024]{1,0:T(8,128)(2,1)} async-done(((bf16[512,1024]{1,0:T(8,128)(2,1)}), bf16[2048,1024]{1,0:T(8,128)(2,1)}) %all-gather.4.cloned.1.call-update) | async-done | bytes 4194320 | tf_op jit(solution)/shard_map/all_gather | solution.py:23
  134.7 13.5 %add_convert_fusion = bf16[2048,1024]{1,0:T(8,128)(2,1)} fusion(f32[2048,1024]{1,0:T(8,128)} %bitcast.9, bf16[2048,1024]{1,0:T(8,128)(2,1)} %param.7, bf16[2048,1024]{1,0:T(8,128)(2,1)} %all-gather.4.cloned.1.call-done, bf16[1024,1024]{1,0:T(8,128)(2,1)} %all-gather.6.cloned.1.call-done), kind=kOutput, calls=%fused_computation | convolution fusion | flops 4305453056 | bytes 23068672 | tf_op jit(solution)/shard_map/dot_general | solution.py:22
  (5 shorter events, 0.1 us)
Async XLA Ops:
  6.5 48.3 %copy-start = (f32[512,1024]{1,0:T(8,128)S(1)}, f32[512,1024]{1,0:T(8,128)}, u32[]{:S(2)}) copy-start(f32[512,1024]{1,0:T(8,128)} %param.6) | copy-start | bytes 6291460
  6.5 49.6 %copy-start.1 = (s32[4,2]{0,1:T(2,128)S(1)}, s32[4,2]{0,1:T(2,128)}, u32[]{:S(2)}) copy-start(s32[4,2]{0,1:T(2,128)} %param.9) | copy-start | bytes 100
  6.5 93.6 %all-gather.6.cloned.1.call-start = ((), (), s32[]{:S(2)}) async-start(), calls=%async_computation.1 | async-start | bytes 2359296 | tf_op jit(solution)/shard_map/all_gather | solution.py:20
  54.8 79.9 %all-gather.4.cloned.1.call-start = ((), (), s32[]{:S(2)}) async-start(), calls=%async_computation | async-start | bytes 5242880 | tf_op jit(solution)/shard_map/all_gather | solution.py:23
Sparse Core Ops, SparseCore 0:
  54.9 45.1 all-gather.5
  101.7 32.9 all-gather.3
